TPU v7x, 32 devices: a whole 2x2x4 slice. The times are simulated.
32 devices in a mesh: gx: 8 (over z, core), gy: 4 (over y, x).
Axes of the slice: x: 2, y: 2, z: 4, core: 2. Of those that a mesh axis runs over, the one named last changes fastest.
Arguments:
- tokens: bfloat16 [512, 4096], P('gx', 'gy'), may hold values from -6 to 6
- gate_blocks: bfloat16 [4, 8, 84, 128, 128], P('gy', 'gx'), may hold values from -0.125 to 0.125
- up_blocks: bfloat16 [4, 8, 84, 128, 128], P('gy', 'gx'), may hold values from -0.125 to 0.125
- gate_coords: int32 [4, 8, 84, 2], P('gy', 'gx'), may hold values from 0 to 13, as said below
- gate_count: int32 [4, 8], P('gy', 'gx'), may hold values from 28 to 84, as said below
- down_blocks: bfloat16 [8, 4, 48, 128, 128], P('gx', 'gy'), may hold values from -0.09375 to 0.09375
- down_rows: int32 [8, 4, 8], P('gx'), may hold values from 0 to 13, as said below
- down_coords: int32 [8, 4, 48, 2], P('gx', 'gy'), may hold values from 0 to 7, as said below
- down_count: int32 [8, 4], P('gx', 'gy'), may hold values from 16 to 48, as said below
Outputs:
- mixed: bfloat16 [512, 4096], P('gx', 'gy')
Inputs may be any that keep to these rules, and one draw needn't show every extreme that they name: `gate_coords`: within each tile the 84 (model-width block, hidden block) pairs are distinct, the first below 8, the second below 14; only the first gate_count slots are live. `gate_count`: some tile has all 84 slots live. `down_rows`: within each down tile the 8 hidden blocks are distinct. `down_coords`: within each down tile the 48 (kept-row index below 8, model-width block below 8) pairs are distinct; only the first down_count slots are live. `down_count`: some tile has all 48 slots live.
All inputs are finite; a program needn't handle non-finite values.
Results may differ from a plain program's by a relative error of at most 0.025.
Values may be sent and summed in bfloat16 or wider, within the bound.
A program may use at most 64 MiB of HBM per device.

v0:
```python
import jax
import jax.numpy as jnp
from jax import lax
from jax.sharding import PartitionSpec as P

FF = 14336
BLOCK = 128


def tile_dense(blocks, coords, count, row_count, col_count):
    live = (jnp.arange(coords.shape[0]) < count).astype(jnp.bfloat16)
    pick = jax.nn.one_hot(coords[:, 0], row_count, dtype=jnp.bfloat16)
    place = jax.nn.one_hot(coords[:, 1], col_count, dtype=jnp.bfloat16) * live[:, None]
    dense = jnp.einsum(
        "sr,sc,skm->rkcm", pick, place, blocks, preferred_element_type=jnp.float32
    ).astype(jnp.bfloat16)
    return dense.reshape(row_count * blocks.shape[1], col_count * blocks.shape[2])


def body(
    tokens,
    gate_blocks,
    up_blocks,
    gate_coords,
    gate_count,
    down_blocks,
    down_rows,
    down_coords,
    down_count,
):
    n_model = tokens.shape[1] // BLOCK
    n_hidden = FF // (BLOCK * lax.axis_size("gx"))
    paired_blocks = jnp.concatenate([gate_blocks[:, 0], up_blocks[:, 0]], -1)
    gathered = lax.all_gather(tokens, "gx", axis=0, tiled=True)
    tok_rows = gathered.shape[0] // lax.axis_size("gy")
    dense_pair = tile_dense(
        paired_blocks[0], gate_coords[0, 0], gate_count[0, 0], n_model, n_hidden
    )
    summed = lax.psum_scatter(
        jnp.dot(gathered, dense_pair, preferred_element_type=jnp.float32).astype(jnp.bfloat16),
        "gy",
        scatter_dimension=0,
        tiled=True,
    ).astype(jnp.float32)
    summed = summed.reshape(tok_rows, n_hidden, 2, BLOCK)
    hidden = (jax.nn.silu(summed[:, :, 0]) * summed[:, :, 1]).astype(jnp.bfloat16)
    kept_count = down_rows.shape[-1]
    dense_down = tile_dense(
        down_blocks[0, 0], down_coords[0, 0], down_count[0, 0], kept_count, n_model
    )
    select_every = jax.nn.one_hot(down_rows[0], n_hidden, dtype=jnp.bfloat16)
    outgoing = jnp.einsum(
        "nfk,guf->gnuk", hidden, select_every, preferred_element_type=jnp.float32
    ).astype(jnp.bfloat16)
    outgoing = outgoing.reshape(outgoing.shape[0], tok_rows, kept_count * BLOCK)
    received = lax.all_to_all(outgoing, "gy", split_axis=0, concat_axis=0, tiled=True)
    kept_all = received.reshape(received.shape[0] * tok_rows, kept_count * BLOCK)
    partial_out = jnp.dot(kept_all, dense_down, preferred_element_type=jnp.float32)
    return lax.psum_scatter(partial_out.astype(jnp.bfloat16), "gx", scatter_dimension=0, tiled=True)


def solution(mesh):
    return jax.shard_map(
        body,
        mesh=mesh,
        in_specs=(
            P("gx", "gy"),
            P("gy", "gx", None, None, None),
            P("gy", "gx", None, None, None),
            P("gy", "gx", None, None),
            P("gy", "gx"),
            P("gx", "gy", None, None, None),
            P("gx", None, None),
            P("gx", "gy", None, None),
            P("gx", "gy"),
        ),
        out_specs=P("gx", "gy"),
        check_vma=False,
    )
```

profile of v0, /device:TPU:0, one launch (start us, length us, event | category | flops | bytes accessed | tf_op | source)
XLA Modules:
  0.0 162.8 jit_solution(1126618621215433886)
XLA Ops:
  6.5 0.0 all-gather.2.cloned.1.call-start
  6.5 0.7 all-gather.2.cloned.1.call-update
  7.3 0.0 reduce-scatter.7.cloned.1.call-start
  7.3 0.8 slice_bitcast_fusion.3
  8.8 6.2 %copy_bitcast_fusion = (bf16[1,84,128,128]{3,1,2,0:T(8,128)(2,1)S(1)}, bf16[1,84,128,128]{3,1,2,0:T(8,128)(2,1)S(1)}) fusion(bf16[1,1,84,128,128]{4,3,2,1,0:T(8,128)(2,1)} %param.11, bf16[1,1,84,128,128]{4,3,2,1,0:T(8,128)(2,1)} %param.10), kind=kLoop, calls=%fused_computation.9 | loop fusion | bytes 11010048 | tf_op jit(solution)/shard_map/squeeze | solution.py:33
  14.9 4.2 %convert_bitcast_fusion = bf16[8,128,14,256]{3,0,1,2:T(8,128)(2,1)} fusion(bf16[1,84,128,128]{3,1,2,0:T(8,128)(2,1)S(1)} %get-tuple-element.11, bf16[1,84,128,128]{3,1,2,0:T(8,128)(2,1)S(1)} %get-tuple-element.12, f32[84,8]{0,1:T(8,128)S(1)} %fusion.39, f32[84,14]{0,1:T(8,128)S(1)} %fusion.38), kind=kOutput, calls=%fused_computation.3 | convolution fusion | flops 631252160 | bytes 12852448 | tf_op jit(solution)/shard_map/sr,sc,skm->rkcm/dot_general | solution.py:14
  19.1 11.4 %copy.24 = bf16[8,128,14,256]{1,0,3,2:T(8,128)(2,1)} copy(bf16[8,128,14,256]{3,0,1,2:T(8,128)(2,1)} %convert_bitcast_fusion) | data formatting | bytes 14680064 | tf_op jit(solution)/shard_map/convert_element_type | solution.py:16
  30.5 3.5 %all-gather.2.cloned.1.call-done = bf16[512,1024]{1,0:T(8,128)(2,1)} async-done(((bf16[64,1024]{1,0:T(8,128)(2,1)}), bf16[512,1024]{1,0:T(8,128)(2,1)}) %all-gather.2.cloned.1.call-update) | async-done | bytes 1048592 | tf_op jit(solution)/shard_map/all_gather | solution.py:34
  33.9 9.2 %fusion.8 = bf16[512,3584]{0,1:T(8,128)(2,1)} fusion(bf16[512,1024]{1,0:T(8,128)(2,1)} %all-gather.2.cloned.1.call-done, bf16[448,8,8,128]{3,2,1,0:T(8,128)(2,1)} %bitcast.103), kind=kOutput, calls=%fused_computation.8 | convolution fusion | flops 3759931392 | bytes 12058624 | tf_op jit(solution)/shard_map/dot_general | solution.py:40
  43.2 5.9 %copy.32 = bf16[512,3584]{1,0:T(8,128)(2,1)} copy(bf16[512,3584]{0,1:T(8,128)(2,1)} %fusion.8) | data formatting | bytes 7340032
  49.1 0.0 copy-start.1
  49.1 0.0 reduce-scatter.7.cloned.1.call-update
  49.7 0.0 copy-done.1
  49.8 47.4 %reduce-scatter.7.cloned.1.call-done = bf16[128,3584]{1,0:T(8,128)(2,1)} async-done(((bf16[512,3584]{1,0:T(8,128)(2,1)}), bf16[128,3584]{1,0:T(8,128)(2,1)}) %reduce-scatter.7.cloned.1.call-update) | async-done | bytes 917520
  97.1 1.5 copy.33
  98.7 0.2 fusion.45
  98.9 0.0 copy-start.2
  98.9 1.4 copy.34
  100.3 0.5 copy.35
  100.8 0.0 copy-done.2
  100.8 1.7 %fusion.19 = bf16[4,128,8,128]{3,2,1,0:T(8,128)(2,1)S(1)} fusion(f32[128,14,1,128]{3,1,0,2:T(8,128)S(1)} %copy.35, f32[128,14,1,128]{3,1,0,2:T(8,128)} %copy.34, s32[4,8]{1,0:T(4,128)S(1)} %bitcast.109), kind=kOutput, calls=%fused_computation.19 | convolution fusion | flops 16581056 | bytes 2883712 | tf_op jit(solution)/shard_map/nfk,guf->gnuk/dot_general | solution.py:52
  102.5 0.0 copy-start
  102.5 1.3 reshape.33
  103.8 3.7 %all-to-all-start = ((bf16[4,128,1024]{2,1,0:T(8,128)(2,1)}), bf16[4,128,1024]{2,1,0:T(8,128)(2,1)S(1)}, u32[]{:S(2)}, u32[]{:S(2)}) async-start(bf16[4,128,1024]{2,1,0:T(8,128)(2,1)} %reshape.33), calls=%async_computation | async-start | bytes 2097152 | tf_op jit(solution)/shard_map/all_to_all | solution.py:56
  107.5 0.0 reduce-scatter.5.cloned.1.call-start
  107.6 0.0 copy-done
  107.6 1.4 convert_bitcast_fusion.1
  109.0 1.4 copy.28
  110.4 10.9 %all-to-all-done = bf16[4,128,1024]{2,1,0:T(8,128)(2,1)S(1)} async-done(((bf16[4,128,1024]{2,1,0:T(8,128)(2,1)}), bf16[4,128,1024]{2,1,0:T(8,128)(2,1)S(1)}, u32[]{:S(2)}, u32[]{:S(2)}) %all-to-all-start) | async-done | bytes 1048608 | tf_op jit(solution)/shard_map/all_to_all | solution.py:56
  121.2 2.2 %fusion.16 = bf16[512,1024]{1,0:T(8,128)(2,1)} fusion(bf16[512,1024]{1,0:T(8,128)(2,1)S(1)} %bitcast.106, bf16[128,8,8,128]{3,2,1,0:T(8,128)(2,1)S(1)} %bitcast.104), kind=kOutput, calls=%fused_computation.18 | convolution fusion | flops 1074266112 | bytes 4194304 | tf_op jit(solution)/shard_map/dot_general | solution.py:58
  123.4 0.0 reduce-scatter.5.cloned.1.call-update
  123.5 32.8 %reduce-scatter.5.cloned.1.call-done = bf16[64,1024]{1,0:T(8,128)(2,1)} async-done(((bf16[512,1024]{1,0:T(8,128)(2,1)}), bf16[64,1024]{1,0:T(8,128)(2,1)}) %reduce-scatter.5.cloned.1.call-update) | async-done | bytes 131088 | tf_op jit(solution)/shard_map/reduce_scatter | solution.py:59
  (7 shorter events, 0.0 us)
Async XLA Ops:
  6.5 27.4 %all-gather.2.cloned.1.call-start = ((), (), s32[]{:S(2)}) async-start(), calls=%async_computation.3 | async-start | bytes 1179648 | tf_op jit(solution)/shard_map/all_gather | solution.py:34
  7.3 89.9 %reduce-scatter.7.cloned.1.call-start = ((), (), s32[]{:S(2)}) async-start(), calls=%async_computation.5 | async-start | bytes 4587520
  49.1 0.7 copy-start.1
  98.9 1.9 %copy-start.2 = (s32[1,4,8]{2,1,0:T(4,128)S(1)}, s32[1,4,8]{2,1,0:T(4,128)}, u32[]{:S(2)}) copy-start(s32[1,4,8]{2,1,0:T(4,128)} %param.15) | copy-start | bytes 388
  102.5 5.1 %copy-start = (bf16[1,1,48,128,128]{4,3,2,1,0:T(8,128)(2,1)S(1)}, bf16[1,1,48,128,128]{4,3,2,1,0:T(8,128)(2,1)}, u32[]{:S(2)}) copy-start(bf16[1,1,48,128,128]{4,3,2,1,0:T(8,128)(2,1)} %param.14) | copy-start | bytes 4718596
  103.8 17.4 %all-to-all-start = ((bf16[4,128,1024]{2,1,0:T(8,128)(2,1)}), bf16[4,128,1024]{2,1,0:T(8,128)(2,1)S(1)}, u32[]{:S(2)}, u32[]{:S(2)}) async-start(bf16[4,128,1024]{2,1,0:T(8,128)(2,1)} %reshape.33), calls=%async_computation | async-start | bytes 2097152 | tf_op jit(solution)/shard_map/all_to_all | solution.py:56
  107.5 48.7 %reduce-scatter.5.cloned.1.call-start = ((), (), s32[]{:S(2)}) async-start(), calls=%async_computation.4 | async-start | bytes 1179648 | tf_op jit(solution)/shard_map/reduce_scatter | solution.py:59
Sparse Core Ops, SparseCore 0:
  8.9 24.9 all-gather.1
  49.2 47.8 reduce-scatter.6
  123.6 32.6 reduce-scatter.4
where the time goes:
time: 163 us
  waiting for transfers between devices  95.2 us (58%)
  local copies, waits for them, and re-layouts  30.5 us (19%)
  matrix products  18.8 us (12%)
  between operations  14.5 us (9%)
  starting transfers between devices  3.78 us (2%)
    unnamed x4, waiting for transfers between devices  48.1 us
    reduce_scatter x1, waiting for transfers between devices, body(): lax.psum_scatter(partial_out.astype(jnp.bfloat16), 'gx', scatter_dimensio...  32.8 us
    convert_element_type x2, local copies, waits for them, and re-layouts, tile_dense(): dense = jnp.einsum('sr,sc,skm->rkcm', pick, place, blocks, preferred_elem...  12.7 us
    all_to_all x1, waiting for transfers between devices, body(): lax.all_to_all(outgoing, 'gy', split_axis=0, concat_axis=0, tiled=True)  10.9 us
    unnamed x10, local copies, waits for them, and re-layouts  9.34 us
    dot_general x1, matrix products, body(): jnp.dot(gathered, dense_pair, preferred_element_type=jnp.float32)  9.24 us
    squeeze x1, local copies, waits for them, and re-layouts, body(): paired_blocks = jnp.concatenate([gate_blocks[:, 0], up_blocks[:, 0]], -1)  6.19 us
    dot_general x2, matrix products, tile_dense(): jnp.einsum('sr,sc,skm->rkcm', pick, place, blocks, preferred_element_type...  5.57 us
  transfers between devices with their start and end apart: 4, of which 4 were waited for; matrix products, arithmetic and copies ran while one was open for 16% of the time, Pallas kernels for 0%

commit v1 on v0

v1 whole, which is shorter than its diff:
```python
import functools

import jax
import jax.numpy as jnp
from jax import lax
from jax.experimental import pallas as pl
from jax.experimental.pallas import tpu as pltpu
from jax.sharding import PartitionSpec as P

BLOCK = 128
FF = 14336
MESH = pl.DeviceIdType.MESH
F32, BF16 = jnp.float32, jnp.bfloat16


def factor(n):
    low = 1
    while low * low * 4 <= n and n % (low * 2) == 0:
        low *= 2
    return n // low, low


def kernel(cfg, tab, tok, gblk, ublk, dblk, out, gw, uw, dw, wd, dd, gat, pa, pb,
           r1a, r1b, s2a, s2b, r2a, r2b, acca, accb, hid, a2s, a2r, ps, fr, facc,
           lsem, gs, gr, s1as, s1ar, s1bs, s1br, s2as, s2ar, s2bs, s2br, xs, xr, fs, fq):
    n_gx, n_gy, n_hi, n_lo, per, nc, rp, rows, n_model, fb, ca, cap, used, capd = cfg
    gx, gy = lax.axis_index("gx"), lax.axis_index("gy")
    zc, mc = gx // per, gx % per
    hi, lo = gy // n_lo, gy % n_lo
    loads = [
        pltpu.make_async_copy(gblk, gw.at[pl.ds(0, cap)], lsem.at[0]),
        pltpu.make_async_copy(ublk, uw.at[pl.ds(0, cap)], lsem.at[1]),
        pltpu.make_async_copy(dblk, dw.at[pl.ds(0, capd)], lsem.at[2]),
    ]
    for load in loads:
        load.start()
    barrier = pltpu.get_barrier_semaphore()
    for d in range(1, n_gy):
        pl.semaphore_signal(barrier, inc=1, device_id=(gx, (gy + d) % n_gy), device_id_type=MESH)
    for d in range(1, n_gx):
        pl.semaphore_signal(barrier, inc=1, device_id=((gx + d) % n_gx, gy), device_id_type=MESH)
    pl.semaphore_wait(barrier, n_gy + n_gx - 2)

    sends = []

    def send(src, dst, ssem, rsem, dev):
        copy = pltpu.make_async_remote_copy(
            src_ref=src, dst_ref=dst, send_sem=ssem, recv_sem=rsem,
            device_id=dev, device_id_type=MESH)
        copy.start()
        sends.append(copy)

    def arrived(ref, sem):
        pltpu.make_async_remote_copy(
            src_ref=ref, dst_ref=ref, send_sem=sem, recv_sem=sem,
            device_id=((gx + 1) % n_gx, gy), device_id_type=MESH).wait_recv()

    for o in range(nc):
        for j in range(per):
            if o == 0 and j == 0:
                continue
            cj = (mc + j) % per
            send(tok, gat.at[o, mc], gs.at[o, j], gr.at[o, mc], ((zc ^ o) * per + cj, gy))
    gat[0, mc] = tok[...]

    gw[cap] = jnp.zeros((BLOCK, BLOCK), BF16)
    uw[cap] = jnp.zeros((BLOCK, BLOCK), BF16)
    dw[capd] = jnp.zeros((BLOCK, BLOCK), BF16)
    loads[0].wait()
    loads[1].wait()

    def dense_col(c, _):
        at = pl.multiple_of(c * 2 * BLOCK, 2 * BLOCK)
        for r in range(n_model):
            slot = tab[r * fb + c]
            wd[pl.ds(r * BLOCK, BLOCK), pl.ds(at, BLOCK)] = gw[slot]
            wd[pl.ds(r * BLOCK, BLOCK), pl.ds(at + BLOCK, BLOCK)] = uw[slot]
        return 0

    lax.fori_loop(0, fb, dense_col, 0)
    down_at, rows_at = n_model * fb, n_model * fb + used * n_model

    def dense_down():
        loads[2].wait()

        def one(c, _):
            at = pl.multiple_of(c * BLOCK, BLOCK)
            for r in range(used):
                slot = tab[down_at + r * n_model + c]
                dd[pl.ds(r * BLOCK, BLOCK), pl.ds(at, BLOCK)] = dw[slot]
            return 0

        lax.fori_loop(0, n_model, one, 0)

    tall = per * rows

    def project(k):
        for j in range(per):
            if k == 0 and j == 0:
                continue
            c = (mc + j) % per
            arrived(gat.at[k, c], gr.at[k, c])
        for part, first, many in ((pa, 0, ca), (pb, ca, fb - ca)):
            def col(c, _, part=part, first=first):
                to = pl.multiple_of(c * 2 * BLOCK, 2 * BLOCK)
                at = pl.multiple_of((c + first) * 2 * BLOCK, 2 * BLOCK)
                y = jnp.dot(gat[k].reshape(tall, n_model * BLOCK),
                            wd[:, pl.ds(at, 2 * BLOCK)], preferred_element_type=F32)
                part[k, :, :, :, pl.ds(to, 2 * BLOCK)] = y.astype(BF16).reshape(
                    n_hi, n_lo, rp, 2 * BLOCK)
                return 0

            lax.fori_loop(0, many, col, 0)
            if part is pa:
                for d in range(1, n_lo):
                    l2 = (lo + d) % n_lo
                    send(pa.at[k, :, l2], r1a.at[k, d - 1], s1as.at[k, d - 1],
                         s1ar.at[k, d - 1], (gx, hi * n_lo + l2))
            else:
                for d in range(1, n_hi):
                    h2 = (hi + d) % n_hi
                    send(pb.at[k, h2], r1b.at[k, d - 1], s1bs.at[k, d - 1],
                         s1br.at[k, d - 1], (gx, h2 * n_lo + lo))

    def reduce_first(k):
        for d in range(1, n_lo):
            arrived(r1a.at[k, d - 1], s1ar.at[k, d - 1])
        for e in list(range(1, n_hi)) + [0]:
            h2 = (hi + e) % n_hi
            s = pa[k, h2, lo].astype(F32)
            for d in range(1, n_lo):
                s = s + r1a[k, d - 1, h2].astype(F32)
            if e == 0:
                acca[k] = s
            else:
                s2a[k, e - 1] = s.astype(BF16)
                send(s2a.at[k, e - 1], r2a.at[k, e - 1], s2as.at[k, e - 1],
                     s2ar.at[k, e - 1], (gx, h2 * n_lo + lo))
        for d in range(1, n_hi):
            arrived(r1b.at[k, d - 1], s1br.at[k, d - 1])
        for e in list(range(1, n_lo)) + [0]:
            l2 = (lo + e) % n_lo
            s = pb[k, hi, l2].astype(F32)
            for d in range(1, n_hi):
                s = s + r1b[k, d - 1, l2].astype(F32)
            if e == 0:
                accb[k] = s
            else:
                s2b[k, e - 1] = s.astype(BF16)
                send(s2b.at[k, e - 1], r2b.at[k, e - 1], s2bs.at[k, e - 1],
                     s2br.at[k, e - 1], (gx, hi * n_lo + l2))

    def activate(k):
        for d in range(1, n_hi):
            arrived(r2a.at[k, d - 1], s2ar.at[k, d - 1])
        for d in range(1, n_lo):
            arrived(r2b.at[k, d - 1], s2br.at[k, d - 1])
        for c in range(fb):
            acc, got, peers, at = (
                (acca, r2a, n_hi, c) if c < ca else (accb, r2b, n_lo, c - ca))
            cols = pl.ds(at * 2 * BLOCK, 2 * BLOCK)
            s = acc[k, :, cols]
            for d in range(1, peers):
                s = s + got[k, d - 1, :, cols].astype(F32)
            gate, up = s[:, :BLOCK], s[:, BLOCK:]
            hid[c] = (gate / (1.0 + jnp.exp(-gate)) * up).astype(BF16)
        for d in list(range(1, n_gy)) + [0]:
            dest = (gy + d) % n_gy
            for q in range(used):
                row = tab[rows_at + dest * used + q]
                cols = pl.ds(q * BLOCK, BLOCK)
                if d == 0:
                    a2r[k, 0, :, cols] = hid[row]
                else:
                    a2s[k, d - 1, :, cols] = hid[row]
            if d:
                send(a2s.at[k, d - 1], a2r.at[k, d], xs.at[k, d - 1],
                     xr.at[k, d - 1], (gx, dest))

    wide = 2 * BLOCK

    def mix(k):
        for d in range(1, n_gy):
            arrived(a2r.at[k, d], xr.at[k, d - 1])

        def col(c, _):
            at = pl.multiple_of(c * wide, wide)
            y = jnp.dot(a2r[k].reshape(n_gy * rp, used * BLOCK), dd[:, pl.ds(at, wide)],
                        preferred_element_type=F32).astype(BF16)
            for d in range(n_gy):
                own = (gy + n_gy - d) % n_gy
                ps[k, pl.ds(pl.multiple_of(own * rp, rp), rp), pl.ds(at, wide)] = (
                    y[d * rp:(d + 1) * rp])
            return 0

        lax.fori_loop(0, n_model * BLOCK // wide, col, 0)
        for j in range(per):
            if k == 0 and j == 0:
                continue
            cj = (mc + j) % per
            send(ps.at[k, pl.ds(pl.multiple_of(cj * rows, rows), rows)], fr.at[k, mc],
                 fs.at[k, j], fq.at[k, mc], ((zc ^ k) * per + cj, gy))
        if k == 0:
            facc[...] = ps[0, pl.ds(pl.multiple_of(mc * rows, rows), rows)].astype(F32)

    for s in range(nc + 3):
        if s < nc:
            project(s)
        if s == 1 or (nc == 1 and s == 0):
            dense_down()
        if 0 <= s - 1 < nc:
            reduce_first(s - 1)
        if 0 <= s - 2 < nc:
            activate(s - 2)
        if 0 <= s - 3 < nc:
            mix(s - 3)

    for k in range(nc):
        for j in range(per):
            if k == 0 and j == 0:
                continue
            c = (mc + j) % per
            arrived(fr.at[k, c], fq.at[k, c])
            facc[...] += fr[k, c].astype(F32)
    out[...] = facc[...].astype(BF16)
    for copy in sends:
        copy.wait_send()


def inverse(coords, count, row_count, col_count):
    slots = coords.shape[0]
    slot = jnp.arange(slots, dtype=jnp.int32)
    place = coords[:, 0] * col_count + coords[:, 1]
    spot = jnp.arange(row_count * col_count, dtype=jnp.int32)
    hit = (place[:, None] == spot[None, :]) & (slot < count)[:, None]
    return jnp.min(jnp.where(hit, slot[:, None], slots), axis=0)


def solution(mesh):
    n_gx, n_gy = mesh.shape["gx"], mesh.shape["gy"]
    n_hi, n_lo = factor(n_gy)
    per = 2 if n_gx % 2 == 0 else 1
    nc = n_gx // per

    def body(tokens, gate_blocks, up_blocks, gate_coords, gate_count,
             down_blocks, down_rows, down_coords, down_count):
        rows, width = tokens.shape
        n_model = width // BLOCK
        fb = FF // (BLOCK * n_gx)
        ca = (fb + 1) // 2
        cb = fb - ca
        cap, capd, used = gate_blocks.shape[2], down_blocks.shape[2], down_rows.shape[-1]
        rp = per * rows // n_gy
        tab = jnp.concatenate([
            inverse(gate_coords[0, 0], gate_count[0, 0], n_model, fb),
            inverse(down_coords[0, 0], down_count[0, 0], used, n_model),
            down_rows.reshape(-1),
        ])
        cfg = (n_gx, n_gy, n_hi, n_lo, per, nc, rp, rows, n_model, fb, ca, cap, used, capd)
        wa, wb = ca * 2 * BLOCK, cb * 2 * BLOCK
        kl, kh, kg = max(n_lo - 1, 1), max(n_hi - 1, 1), max(n_gy - 1, 1)
        vm, dma = pltpu.VMEM, pltpu.SemaphoreType.DMA
        hbm = pl.BlockSpec(memory_space=pltpu.HBM)
        return pl.pallas_call(
            functools.partial(kernel, cfg),
            out_shape=jax.ShapeDtypeStruct((rows, width), BF16),
            in_specs=[
                pl.BlockSpec(memory_space=pltpu.SMEM),
                pl.BlockSpec(memory_space=pltpu.VMEM),
                hbm, hbm, hbm,
            ],
            out_specs=pl.BlockSpec(memory_space=pltpu.VMEM),
            scratch_shapes=[
                vm((cap + 1, BLOCK, BLOCK), BF16),
                vm((cap + 1, BLOCK, BLOCK), BF16),
                vm((capd + 1, BLOCK, BLOCK), BF16),
                vm((width, fb * 2 * BLOCK), BF16),
                vm((used * BLOCK, width), BF16),
                vm((nc, per, rows, width), BF16),
                vm((nc, n_hi, n_lo, rp, wa), BF16),
                vm((nc, n_hi, n_lo, rp, wb), BF16),
                vm((nc, kl, n_hi, rp, wa), BF16),
                vm((nc, kh, n_lo, rp, wb), BF16),
                vm((nc, kh, rp, wa), BF16),
                vm((nc, kl, rp, wb), BF16),
                vm((nc, kh, rp, wa), BF16),
                vm((nc, kl, rp, wb), BF16),
                vm((nc, rp, wa), F32),
                vm((nc, rp, wb), F32),
                vm((fb, rp, BLOCK), BF16),
                vm((nc, kg, rp, used * BLOCK), BF16),
                vm((nc, n_gy, rp, used * BLOCK), BF16),
                vm((nc, per * rows, width), BF16),
                vm((nc, per, rows, width), BF16),
                vm((rows, width), F32),
                dma((3,)),
                dma((nc, per)), dma((nc, per)),
                dma((nc, kl)), dma((nc, kl)),
                dma((nc, kh)), dma((nc, kh)),
                dma((nc, kh)), dma((nc, kh)),
                dma((nc, kl)), dma((nc, kl)),
                dma((nc, kg)), dma((nc, kg)),
                dma((nc, per)), dma((nc, per)),
            ],
            compiler_params=pltpu.CompilerParams(
                collective_id=0, has_side_effects=True, vmem_limit_bytes=60 * 1024 * 1024),
        )(tab, tokens, gate_blocks.reshape(cap, BLOCK, BLOCK),
          up_blocks.reshape(cap, BLOCK, BLOCK), down_blocks.reshape(capd, BLOCK, BLOCK))

    return jax.shard_map(
        body,
        mesh=mesh,
        in_specs=(
            P("gx", "gy"),
            P("gy", "gx", None, None, None),
            P("gy", "gx", None, None, None),
            P("gy", "gx", None, None),
            P("gy", "gx"),
            P("gx", "gy", None, None, None),
            P("gx", None, None),
            P("gx", "gy", None, None),
            P("gx", "gy"),
        ),
        out_specs=P("gx", "gy"),
        check_vma=False,
    )
```

time: 163 us -> 83.3 us (0.51)
  the two profiles are of different devices: /device:TPU:0 before, /device:TPU:16 now
where the time goes in v1:
time: 83.3 us; the launch traced here: 83.1 us
  Pallas kernels  77 us (92%)
  other arithmetic  2.38 us (3%)
  local copies, waits for them, and re-layouts  2.33 us (3%)
  between operations  1.32 us (2%)
    pallas_call x1, Pallas kernels, body(): pl.pallas_call(functools.partial(kernel, cfg), out_shape=jax.ShapeDtypeSt...  77 us

profile of v1, /device:TPU:16, one launch (start us, length us, event | category | flops | bytes accessed | tf_op | source)
XLA Modules:
  0.0 83.1 jit_solution(15708841861534308456)
XLA Ops:
  1.3 0.8 add_bitcast_fusion.1
  2.1 0.1 select_reduce_fusion
  2.2 0.8 reshape.20
  3.0 0.8 add_bitcast_fusion
  3.7 0.1 select_reduce_fusion.1
  3.8 0.6 pad_add_fusion.tab
  4.5 77.0 %shard_map.91 = bf16[64,1024]{1,0:T(8,128)(2,1)} custom-call(s32[208]{0:T(256)} %pad_add_fusion.tab, bf16[64,1024]{1,0:T(8,128)(2,1)} %tok.1, bf16[84,128,128]{2,1,0:T(8,128)(2,1)} %bitcast.13, bf16[84,128,128]{2,1,0:T(8,128)(2,1)} %bitcast.14, bf16[48,128,128]{2,1,0:T(8,128)(2,1)} %bitcast.15), custom_call_target="tpu_custom_call" | custom-call | tf_op jit(solution)/shard_map/pallas_call | solution.py:264
  81.5 1.6 %copy.13 = bf16[64,1024]{1,0:T(8,128)(2,1)} copy(bf16[64,1024]{1,0:T(8,128)(2,1)} %shard_map.91) | data formatting | bytes 262144
  (2 shorter events, 0.0 us)

commit v2 on v1

--- a/solution.py
+++ b/solution.py
@@ -20,9 +20,9 @@
     return n // low, low
 
 
-def kernel(cfg, tab, tok, gblk, ublk, dblk, out, gw, uw, dw, wd, dd, gat, pa, pb,
-           r1a, r1b, s2a, s2b, r2a, r2b, acca, accb, hid, a2s, a2r, ps, fr, facc,
-           lsem, gs, gr, s1as, s1ar, s1bs, s1br, s2as, s2ar, s2bs, s2br, xs, xr, fs, fq):
+def kernel(cfg, tab, downs, kept, tok, gblk, ublk, dblk, out, gw, uw, dw, gat, pa, pb,
+           r1a, r1b, s2a, s2b, r2a, r2b, acca, accb, hid, a2s, a2r, ps, fp, f2, fr, facc,
+           lsem, gs, gr, s1as, s1ar, s1bs, s1br, s2as, s2ar, s2bs, s2br, xs, xr, fs, fq, fps, fpr):
     n_gx, n_gy, n_hi, n_lo, per, nc, rp, rows, n_model, fb, ca, cap, used, capd = cfg
     gx, gy = lax.axis_index("gx"), lax.axis_index("gy")
     zc, mc = gx // per, gx % per
@@ -55,13 +55,20 @@
             src_ref=ref, dst_ref=ref, send_sem=sem, recv_sem=sem,
             device_id=((gx + 1) % n_gx, gy), device_id_type=MESH).wait_recv()
 
-    for o in range(nc):
-        for j in range(per):
-            if o == 0 and j == 0:
-                continue
-            cj = (mc + j) % per
-            send(tok, gat.at[o, mc], gs.at[o, j], gr.at[o, mc], ((zc ^ o) * per + cj, gy))
+    order = list(range(nc))
+    for j in range(1, per):
+        send(tok, gat.at[0, mc], gs.at[0, j], gr.at[0, mc], (zc * per + (mc + j) % per, gy))
+    for o in order:
+        if o:
+            send(tok, gat.at[o, mc], gs.at[o, 0], gr.at[o, mc], ((zc ^ o) * per + mc, gy))
     gat[0, mc] = tok[...]
+
+    def relay(o):
+        if o:
+            arrived(gat.at[o, mc], gr.at[o, mc])
+            for j in range(1, per):
+                send(gat.at[o, mc], gat.at[o, mc], gs.at[o, j], gr.at[o, mc],
+                     (zc * per + (mc + j) % per, gy))
 
     gw[cap] = jnp.zeros((BLOCK, BLOCK), BF16)
     uw[cap] = jnp.zeros((BLOCK, BLOCK), BF16)
@@ -69,48 +76,25 @@
     loads[0].wait()
     loads[1].wait()
 
-    def dense_col(c, _):
-        at = pl.multiple_of(c * 2 * BLOCK, 2 * BLOCK)
-        for r in range(n_model):
-            slot = tab[r * fb + c]
-            wd[pl.ds(r * BLOCK, BLOCK), pl.ds(at, BLOCK)] = gw[slot]
-            wd[pl.ds(r * BLOCK, BLOCK), pl.ds(at + BLOCK, BLOCK)] = uw[slot]
-        return 0
-
-    lax.fori_loop(0, fb, dense_col, 0)
-    down_at, rows_at = n_model * fb, n_model * fb + used * n_model
-
-    def dense_down():
-        loads[2].wait()
-
-        def one(c, _):
-            at = pl.multiple_of(c * BLOCK, BLOCK)
-            for r in range(used):
-                slot = tab[down_at + r * n_model + c]
-                dd[pl.ds(r * BLOCK, BLOCK), pl.ds(at, BLOCK)] = dw[slot]
-            return 0
-
-        lax.fori_loop(0, n_model, one, 0)
-
     tall = per * rows
 
     def project(k):
-        for j in range(per):
-            if k == 0 and j == 0:
-                continue
+        for j in range(1, per):
             c = (mc + j) % per
             arrived(gat.at[k, c], gr.at[k, c])
         for part, first, many in ((pa, 0, ca), (pb, ca, fb - ca)):
             def col(c, _, part=part, first=first):
                 to = pl.multiple_of(c * 2 * BLOCK, 2 * BLOCK)
-                at = pl.multiple_of((c + first) * 2 * BLOCK, 2 * BLOCK)
-                y = jnp.dot(gat[k].reshape(tall, n_model * BLOCK),
-                            wd[:, pl.ds(at, 2 * BLOCK)], preferred_element_type=F32)
+                slots = [tab[r * fb + c + first] for r in range(n_model)]
+                weight = jnp.concatenate(
+                    [jnp.concatenate([gw[i], uw[i]], axis=1) for i in slots], axis=0)
+                y = jnp.dot(gat[k].reshape(tall, n_model * BLOCK), weight,
+                            preferred_element_type=F32)
                 part[k, :, :, :, pl.ds(to, 2 * BLOCK)] = y.astype(BF16).reshape(
                     n_hi, n_lo, rp, 2 * BLOCK)
                 return 0
 
-            lax.fori_loop(0, many, col, 0)
+            lax.fori_loop(0, many, col, 0, unroll=True)
             if part is pa:
                 for d in range(1, n_lo):
                     l2 = (lo + d) % n_lo
@@ -167,7 +151,7 @@
         for d in list(range(1, n_gy)) + [0]:
             dest = (gy + d) % n_gy
             for q in range(used):
-                row = tab[rows_at + dest * used + q]
+                row = kept[0, dest, q]
                 cols = pl.ds(q * BLOCK, BLOCK)
                 if d == 0:
                     a2r[k, 0, :, cols] = hid[row]
@@ -185,7 +169,11 @@
 
         def col(c, _):
             at = pl.multiple_of(c * wide, wide)
-            y = jnp.dot(a2r[k].reshape(n_gy * rp, used * BLOCK), dd[:, pl.ds(at, wide)],
+            slots = [[downs[r * n_model + c * 2 + i] for i in range(2)]
+                     for r in range(used)]
+            weight = jnp.concatenate(
+                [jnp.concatenate([dw[i] for i in pair], axis=1) for pair in slots], axis=0)
+            y = jnp.dot(a2r[k].reshape(n_gy * rp, used * BLOCK), weight,
                         preferred_element_type=F32).astype(BF16)
             for d in range(n_gy):
                 own = (gy + n_gy - d) % n_gy
@@ -194,34 +182,43 @@
             return 0
 
         lax.fori_loop(0, n_model * BLOCK // wide, col, 0)
-        for j in range(per):
-            if k == 0 and j == 0:
-                continue
+        for j in range(1, per):
             cj = (mc + j) % per
-            send(ps.at[k, pl.ds(pl.multiple_of(cj * rows, rows), rows)], fr.at[k, mc],
-                 fs.at[k, j], fq.at[k, mc], ((zc ^ k) * per + cj, gy))
-        if k == 0:
-            facc[...] = ps[0, pl.ds(pl.multiple_of(mc * rows, rows), rows)].astype(F32)
-
-    for s in range(nc + 3):
+            send(ps.at[k, pl.ds(pl.multiple_of(cj * rows, rows), rows)], fp.at[k, j - 1],
+                 fps.at[k, j - 1], fpr.at[k, j - 1], (zc * per + cj, gy))
+
+    def finish(k):
+        s = ps[k, pl.ds(pl.multiple_of(mc * rows, rows), rows)].astype(F32)
+        for j in range(1, per):
+            arrived(fp.at[k, j - 1], fpr.at[k, j - 1])
+            s = s + fp[k, j - 1].astype(F32)
+        if k:
+            f2[k] = s.astype(BF16)
+            send(f2.at[k], fr.at[k], fs.at[k], fq.at[k], ((zc ^ k) * per + mc, gy))
+        else:
+            facc[...] = s
+
+    relay(order[0])
+    for s in range(nc + 4):
         if s < nc:
-            project(s)
-        if s == 1 or (nc == 1 and s == 0):
-            dense_down()
+            project(order[s])
+        if s + 1 < nc:
+            relay(order[s + 1])
+        if s == 0:
+            loads[2].wait()
         if 0 <= s - 1 < nc:
-            reduce_first(s - 1)
+            reduce_first(order[s - 1])
+        if 0 <= s - 4 < nc:
+            finish(order[s - 4])
         if 0 <= s - 2 < nc:
-            activate(s - 2)
+            activate(order[s - 2])
         if 0 <= s - 3 < nc:
-            mix(s - 3)
-
-    for k in range(nc):
-        for j in range(per):
-            if k == 0 and j == 0:
-                continue
-            c = (mc + j) % per
-            arrived(fr.at[k, c], fq.at[k, c])
-            facc[...] += fr[k, c].astype(F32)
+            mix(order[s - 3])
+
+    for k in order:
+        if k:
+            arrived(fr.at[k], fq.at[k])
+            facc[...] += fr[k].astype(F32)
     out[...] = facc[...].astype(BF16)
     for copy in sends:
         copy.wait_send()
@@ -251,11 +248,8 @@
         cb = fb - ca
         cap, capd, used = gate_blocks.shape[2], down_blocks.shape[2], down_rows.shape[-1]
         rp = per * rows // n_gy
-        tab = jnp.concatenate([
-            inverse(gate_coords[0, 0], gate_count[0, 0], n_model, fb),
-            inverse(down_coords[0, 0], down_count[0, 0], used, n_model),
-            down_rows.reshape(-1),
-        ])
+        tab = inverse(gate_coords[0, 0], gate_count[0, 0], n_model, fb)
+        downs = inverse(down_coords[0, 0], down_count[0, 0], used, n_model)
         cfg = (n_gx, n_gy, n_hi, n_lo, per, nc, rp, rows, n_model, fb, ca, cap, used, capd)
         wa, wb = ca * 2 * BLOCK, cb * 2 * BLOCK
         kl, kh, kg = max(n_lo - 1, 1), max(n_hi - 1, 1), max(n_gy - 1, 1)
@@ -266,6 +260,8 @@
             out_shape=jax.ShapeDtypeStruct((rows, width), BF16),
             in_specs=[
                 pl.BlockSpec(memory_space=pltpu.SMEM),
+                pl.BlockSpec(memory_space=pltpu.SMEM),
+                pl.BlockSpec(memory_space=pltpu.SMEM),
                 pl.BlockSpec(memory_space=pltpu.VMEM),
                 hbm, hbm, hbm,
             ],
@@ -274,8 +270,6 @@
                 vm((cap + 1, BLOCK, BLOCK), BF16),
                 vm((cap + 1, BLOCK, BLOCK), BF16),
                 vm((capd + 1, BLOCK, BLOCK), BF16),
-                vm((width, fb * 2 * BLOCK), BF16),
-                vm((used * BLOCK, width), BF16),
                 vm((nc, per, rows, width), BF16),
                 vm((nc, n_hi, n_lo, rp, wa), BF16),
                 vm((nc, n_hi, n_lo, rp, wb), BF16),
@@ -291,7 +285,9 @@
                 vm((nc, kg, rp, used * BLOCK), BF16),
                 vm((nc, n_gy, rp, used * BLOCK), BF16),
                 vm((nc, per * rows, width), BF16),
-                vm((nc, per, rows, width), BF16),
+                vm((nc, max(per - 1, 1), rows, width), BF16),
+                vm((nc, rows, width), BF16),
+                vm((nc, rows, width), BF16),
                 vm((rows, width), F32),
                 dma((3,)),
                 dma((nc, per)), dma((nc, per)),
@@ -300,11 +296,12 @@
                 dma((nc, kh)), dma((nc, kh)),
                 dma((nc, kl)), dma((nc, kl)),
                 dma((nc, kg)), dma((nc, kg)),
-                dma((nc, per)), dma((nc, per)),
+                dma((nc,)), dma((nc,)),
+                dma((nc, max(per - 1, 1))), dma((nc, max(per - 1, 1))),
             ],
             compiler_params=pltpu.CompilerParams(
                 collective_id=0, has_side_effects=True, vmem_limit_bytes=60 * 1024 * 1024),
-        )(tab, tokens, gate_blocks.reshape(cap, BLOCK, BLOCK),
+        )(tab, downs, down_rows, tokens, gate_blocks.reshape(cap, BLOCK, BLOCK),
           up_blocks.reshape(cap, BLOCK, BLOCK), down_blocks.reshape(capd, BLOCK, BLOCK))
 
     return jax.shard_map(

time: 83.3 us -> 69.8 us (0.84)
  the two profiles are of different devices: /device:TPU:16 before, /device:TPU:0 now
where the time goes in v2:
time: 69.8 us; the launch traced here: 68.7 us
  Pallas kernels  63.1 us (90%)
  other arithmetic  2.75 us (4%)
  local copies, waits for them, and re-layouts  1.57 us (2%)
  between operations  1.32 us (2%)
    pallas_call x1, Pallas kernels, body(): pl.pallas_call(functools.partial(kernel, cfg), out_shape=jax.ShapeDtypeSt...  63.1 us
    unnamed x1, local copies, waits for them, and re-layouts  1.57 us
    eq x2, other arithmetic, inverse(): hit = (place[:, None] == spot[None, :]) & (slot < count)[:, None]  1.52 us

profile of v2, /device:TPU:0, one launch (start us, length us, event | category | flops | bytes accessed | tf_op | source)
XLA Modules:
  0.0 68.7 jit_solution(7188546672986369437)
XLA Ops:
  1.3 0.8 %add_bitcast_fusion.1 = s32[84]{0:T(128)S(1)} fusion(s32[84,2]{0,1:T(2,128)} %bitcast.16), kind=kLoop, calls=%fused_computation.9 | loop fusion | flops 168 | bytes 1008 | tf_op jit(solution)/shard_map/eq | solution.py:232
  2.1 0.6 select_reduce_fusion.tab
  2.7 0.8 %add_bitcast_fusion = s32[48]{0:T(128)S(1)} fusion(s32[48,2]{0,1:T(2,128)} %bitcast.17), kind=kLoop, calls=%fused_computation.7 | loop fusion | flops 96 | bytes 576 | tf_op jit(solution)/shard_map/eq | solution.py:232
  3.5 0.6 select_reduce_fusion.1.downs
  4.1 63.1 %shard_map.91 = bf16[64,1024]{1,0:T(8,128)(2,1)} custom-call(s32[112]{0:T(128)} %select_reduce_fusion.tab, s32[64]{0:T(128)} %select_reduce_fusion.1.downs, s32[1,4,8]{2,1,0:T(4,128)} %kept.1, bf16[64,1024]{1,0:T(8,128)(2,1)} %tok.1, bf16[84,128,128]{2,1,0:T(8,128)(2,1)} %bitcast.13, bf16[84,128,128]{2,1,0:T(8,128)(2,1)} %bitcast.14, ...), custom_call_target="tpu_custom_call" | custom-call | tf_op jit(solution)/shard_map/pallas_call | solution.py:258
  67.2 1.6 %copy.13 = bf16[64,1024]{1,0:T(8,128)(2,1)} copy(bf16[64,1024]{1,0:T(8,128)(2,1)} %shard_map.91) | data formatting | bytes 262144
  (2 shorter events, 0.0 us)
